TPU v7x, 256 devices: a whole 4x4x8 slice. The times are simulated.
256 devices in a mesh: batch: 8 (over x, core), cache: 32 (over y, z).
Axes of the slice: x: 4, y: 4, z: 8, core: 2. Of those that a mesh axis runs over, the one named last changes fastest.
Arguments:
- hidden_in: bfloat16 [64, 4096], P('batch'), may hold values from -6 to 6
- attn_gain: bfloat16 [4096], replicated, may hold values from 0.25 to 1.75
- w_query: bfloat16 [4096, 4096], P(None, 'cache'), may hold values from -0.09375 to 0.09375
- w_key: bfloat16 [4096, 1024], P(None, 'cache'), may hold values from -0.09375 to 0.09375
- w_value: bfloat16 [4096, 1024], P(None, 'cache'), may hold values from -0.09375 to 0.09375
- key_cache: bfloat16 [64, 4096, 1024], P('batch', 'cache'), may hold values from -400 to 400, as said below
- value_cache: bfloat16 [64, 4096, 1024], P('batch', 'cache'), may hold values from -6 to 6
- write_pos: int32 [64], P('batch'), may hold values from 0 to 12287, as said below
- cache_len: int32 [64], P('batch'), may hold values from 0 to 4095, as said below
- w_out: bfloat16 [4096, 4096], P('cache'), may hold values from -0.1875 to 0.1875
- mlp_gain: bfloat16 [4096], replicated, may hold values from 0.25 to 1.75
- w_gate: bfloat16 [4096, 7168], P(None, 'cache'), may hold values from -0.09375 to 0.09375
- w_up: bfloat16 [4096, 7168], P(None, 'cache'), may hold values from -0.09375 to 0.09375
- w_down: bfloat16 [7168, 4096], P('cache'), may hold values from -0.125 to 0.125
Outputs:
- hidden_out: bfloat16 [64, 4096], P('batch', 'cache')
Inputs may be any that keep to these rules, and one draw needn't show every extreme that they name: `key_cache`: keys of earlier tokens are finite reals. `write_pos`: positions of the new tokens; the largest value occurs in every draw. cache_len never exceeds write_pos; both 0 and 4095 occur in every draw, and many sequences attend fewer than 4095 earlier tokens.
All inputs are finite; a program needn't handle non-finite values.
Results may differ from a plain program's by a relative error of at most 0.017.
Values may be sent and summed in bfloat16 or wider, within the bound.
A program may use at most 64 MiB of HBM per device.

v0:
```python
import jax
import jax.numpy as jnp
from jax import lax
from jax.sharding import PartitionSpec as P

HEADS = 32
KV_HEADS = 8
HEAD_DIM = 128


def sent_together(arrays, axis, dim, along):
    widths = [a.shape[along] for a in arrays]
    both = jnp.concatenate(arrays, axis=along)
    out = lax.all_gather(both, axis, axis=dim, tiled=True)
    return tuple(jnp.split(out, [sum(widths[:k]) for k in range(1, len(widths))], axis=along))


def sent_to_all(x, axis):
    copies = jnp.broadcast_to(x, (lax.axis_size(axis), *x.shape))
    return lax.all_to_all(copies, axis, split_axis=0, concat_axis=0, tiled=True)


def of_everyone(x, axis):
    return sent_to_all(x, axis).max(axis=0)


def over_copies(x, axis):
    return sent_to_all(x, axis).sum(axis=0)


def cut_along(x, dim, devices):
    before, after = (x.shape[:dim], x.shape[dim + 1 :])
    return jnp.moveaxis(x.reshape(*before, devices, -1, *after), dim, 0)


def sum_at_owner(x, axis, dim):
    devices = lax.axis_size(axis)
    parts = lax.all_to_all(cut_along(x, dim, devices), axis, 0, 0, tiled=True)
    return jnp.sum(parts.astype(jnp.float32), axis=0)


def laid_out(parts, dim):
    parts = jnp.moveaxis(parts, 0, dim)
    lengths = parts.shape
    return parts.reshape(*lengths[:dim], lengths[dim] * lengths[dim + 1], *lengths[dim + 2 :])


def gather_directly(x, axis, dim):
    parts = sent_to_all(x, axis)
    return laid_out(parts, dim)


def rms_norm(values, gain):
    wide = values.astype(jnp.float32)
    spread = jnp.mean(wide * wide, axis=-1, keepdims=True)
    return (wide * lax.rsqrt(spread + 1e-05) * gain.astype(jnp.float32)).astype(jnp.bfloat16)


def rotate(heads, position):
    half = heads.shape[-1] // 2
    freq = 10000.0 ** (-(jnp.arange(half, dtype=jnp.float32) * 2.0 / heads.shape[-1]))
    angle = position.astype(jnp.float32)[:, None] * freq[None, :]
    cosine = jnp.cos(angle)[:, None, :]
    sine = jnp.sin(angle)[:, None, :]
    first = heads[..., :half]
    second = heads[..., half:]
    return jnp.concatenate(
        [first * cosine - second * sine, second * cosine + first * sine], axis=-1
    )


def per_device(
    hidden_in,
    attn_gain,
    w_query,
    w_key,
    w_value,
    key_cache,
    value_cache,
    write_pos,
    cache_len,
    w_out,
    mlp_gain,
    w_gate,
    w_up,
    w_down,
):
    seqs = hidden_in.shape[0]
    embedding_width = hidden_in.shape[1]
    ncache = lax.axis_size("cache")
    position_index = lax.axis_index("cache")
    slots_dev = key_cache.shape[1]
    window = slots_dev * ncache
    group = HEADS // KV_HEADS
    scale = 1.0 / HEAD_DIM**0.5
    feature_width = embedding_width // ncache
    normed = rms_norm(hidden_in, attn_gain)
    query_slice = jnp.dot(normed, w_query, preferred_element_type=jnp.float32).astype(jnp.bfloat16)
    key_part = jnp.dot(normed, w_key, preferred_element_type=jnp.float32).astype(jnp.bfloat16)
    value_part = jnp.dot(normed, w_value, preferred_element_type=jnp.float32).astype(jnp.bfloat16)
    query_raw, key_raw, value_new = (
        lax.all_gather(query_slice, "cache", axis=1, tiled=True),
        *sent_together((key_part, value_part), "cache", 1, 0),
    )
    query = rotate(query_raw.astype(jnp.float32).reshape(seqs, HEADS, HEAD_DIM), write_pos).astype(
        jnp.bfloat16
    )
    fresh_key_row = rotate(
        key_raw.astype(jnp.float32).reshape(seqs, KV_HEADS, HEAD_DIM), write_pos
    ).astype(jnp.bfloat16)
    value_heads = value_new.reshape(seqs, KV_HEADS, HEAD_DIM)
    slots = position_index * slots_dev + jnp.arange(slots_dev, dtype=jnp.int32)
    dist = (write_pos[:, None] - 1 - slots[None, :]) % window + 1
    valid = dist <= cache_len[:, None]
    owner = write_pos % window // slots_dev == position_index
    query_head_group = query.reshape(seqs, KV_HEADS, group, HEAD_DIM)
    keys = key_cache.reshape(seqs, slots_dev, KV_HEADS, HEAD_DIM)
    values = value_cache.reshape(seqs, slots_dev, KV_HEADS, HEAD_DIM)
    scores = (
        jnp.einsum("bkgd,bwkd->bkgw", query_head_group, keys, preferred_element_type=jnp.float32)
        * scale
    )
    own = (
        jnp.einsum(
            "vyjf,vyf->vyj", query_head_group, fresh_key_row, preferred_element_type=jnp.float32
        )
        * scale
    )
    scores = jnp.where(valid[:, None, None, :], scores, -1e30)
    own = jnp.where(owner[:, None, None], own, -1e30)
    top = jnp.maximum(jnp.max(scores, axis=-1), own)
    weights = jnp.where(valid[:, None, None, :], jnp.exp(scores - top[..., None]), 0.0)
    own_weight = jnp.where(owner[:, None, None], jnp.exp(own - top), 0.0)
    total = jnp.sum(weights, axis=-1) + own_weight
    own_low = lax.optimization_barrier(own_weight.astype(jnp.bfloat16)).astype(jnp.float32)
    reduced_total = jnp.einsum(
        "bkgw,bwkd->bkgd", weights.astype(jnp.bfloat16), values, preferred_element_type=jnp.float32
    )
    reduced_total = (
        reduced_total + own_low[..., None] * value_heads.astype(jnp.float32)[:, :, None, :]
    )
    top_flat = top.reshape(seqs, HEADS)
    total_flat = total.reshape(seqs, HEADS)
    summed_flat = reduced_total.reshape(seqs, HEADS, HEAD_DIM)
    largest = of_everyone(top_flat, "cache")
    factor = jnp.exp(top_flat - largest)
    scaled_total = over_copies(total_flat * factor, "cache")
    scaled_sum = (summed_flat * factor[..., None]).reshape(seqs, HEADS * HEAD_DIM)
    local_partial_sum = sum_at_owner(scaled_sum.astype(jnp.bfloat16), "cache", 1)
    total_features = jnp.repeat(scaled_total, HEAD_DIM, axis=1)
    own_total = lax.dynamic_slice_in_dim(
        total_features, position_index * feature_width, feature_width, 1
    )
    attended = (local_partial_sum / own_total).astype(jnp.bfloat16)
    projected = jnp.dot(attended, w_out, preferred_element_type=jnp.float32)
    share = sum_at_owner(projected.astype(jnp.bfloat16), "cache", 1)
    hidden_share = lax.dynamic_slice_in_dim(
        hidden_in, position_index * feature_width, feature_width, 1
    )
    mid_own = (hidden_share.astype(jnp.float32) + share).astype(jnp.bfloat16)
    mid_wide = mid_own.astype(jnp.float32)
    squares = over_copies(jnp.sum(mid_wide * mid_wide, axis=-1), "cache")
    gain_share = lax.dynamic_slice_in_dim(
        mlp_gain, position_index * feature_width, feature_width, 0
    )
    normed_share = (
        mid_wide
        * lax.rsqrt(squares / embedding_width + 1e-05)[:, None]
        * gain_share.astype(jnp.float32)
    ).astype(jnp.bfloat16)
    normed_mid = gather_directly(normed_share, "cache", 1)
    gate = jnp.dot(normed_mid, w_gate, preferred_element_type=jnp.float32)
    upper = jnp.dot(normed_mid, w_up, preferred_element_type=jnp.float32)
    act = (jax.nn.silu(gate) * upper).astype(jnp.bfloat16)
    down = jnp.dot(act, w_down, preferred_element_type=jnp.float32)
    down_own = sum_at_owner(down.astype(jnp.bfloat16), "cache", 1)
    return (mid_own.astype(jnp.float32) + down_own).astype(jnp.bfloat16)


def solution(mesh):
    in_specs = (
        P("batch", None),
        P(),
        P(None, "cache"),
        P(None, "cache"),
        P(None, "cache"),
        P("batch", "cache", None),
        P("batch", "cache", None),
        P("batch"),
        P("batch"),
        P("cache", None),
        P(),
        P(None, "cache"),
        P(None, "cache"),
        P("cache", None),
    )
    out_specs = P("batch", "cache")
    return jax.shard_map(
        per_device, mesh=mesh, in_specs=in_specs, out_specs=out_specs, check_vma=False
    )
```

profile of v0, /device:TPU:4, one launch (start us, length us, event | category | flops | bytes accessed | tf_op | source)
XLA Modules:
  0.0 211.6 jit_solution(16157100261924183315)
XLA Ops:
  0.0 0.0 copy-start
  0.0 0.0 copy-start.2
  0.0 0.8 fusion.62
  0.8 0.7 fusion.52
  1.5 1.0 fusion.18
  2.5 0.7 convert_element_type.92
  3.2 1.2 convolution_convert_fusion.3
  4.5 1.2 convolution_convert_fusion.2
  5.7 1.6 convolution_convert_fusion.4
  7.3 52.3 %all_gather.6 = bf16[8,4096]{1,0:T(8,128)(2,1)S(1)} all-gather(bf16[8,128]{1,0:T(8,128)(2,1)S(1)} %convolution_convert_fusion.4), channel_id=1, replica_groups=mesh['batch'=8,'cache'=32] {'cache'}, dimensions={1}, use_global_device_ids=true | all-gather | bytes 67584 | tf_op jit(solution)/shard_map/all_gather | solution.py:102
  59.6 0.1 multiply_cosine_fusion
  59.7 0.1 subtract_convert_fusion
  59.9 42.2 %all-gather = bf16[32,32,16]{1,2,0:T(8,128)(2,1)S(1)} all-gather(bf16[1,32,16]{1,2,0:T(8,128)(2,1)S(1)} %maximum_bitcast_fusion.1), channel_id=1, replica_groups=mesh['batch'=8,'cache'=32] {'cache'}, dimensions={0}, use_global_device_ids=true | all-gather | bytes 33792 | tf_op jit(solution)/shard_map/all_gather | solution.py:14
  102.2 0.2 reshape.209
  102.4 0.1 subtract_convert_fusion.1
  102.4 0.1 maximum_bitcast_fusion
  102.5 0.0 copy-done.2
  102.5 0.1 fusion.44
  102.6 0.3 fusion.33
  102.9 0.0 copy-done
  102.9 1.3 fusion.63
  104.2 0.1 fusion.35
  104.3 0.1 copy.61
  104.4 0.1 copy.63
  104.5 0.7 reshape.212
  105.2 5.7 %all-to-all-start = ((f32[32,1,256]{2,1,0:T(1,128)}), f32[32,1,256]{2,1,0:T(1,128)S(1)}, u32[]{:S(2)}, u32[]{:S(2)}) async-start(f32[32,1,256]{2,1,0:T(1,128)} %reshape.212), calls=%async_computation | async-start | bytes 65536 | tf_op jit(solution)/shard_map/all_to_all | solution.py:20
  110.9 0.3 fusion.22
  111.2 0.1 fusion.56
  111.3 0.0 copy-start.1
  111.3 2.4 %fusion.12 = f32[8,8,4,128]{3,2,1,0:T(4,128)S(1)} fusion(f32[8,8,4,128]{3,2,1,0:T(4,128)S(1)} %get-tuple-element.22, f32[8,8,128]{2,1,0:T(8,128)S(1)} %copy.60, f32[8,8,4]{2,1,0:T(8,128)S(1)} %convert_element_type.100, f32[8,8,4]{2,1,0:T(8,128)S(1)} %fusion.35, pred[8,128]{1,0:T(8,128)(4,1)S(1)} %fusion.44, bf16[8,128,1024]{2,1,0:T(8,128)(2,1)} %param.20), kind=kOutput, calls=%fused_computation.10 | convolution fusion | flops 8552448 | bytes 2395136 | tf_op jit(solution)/shard_map/bkgw,bwkd->bkgd/dot_general | solution.py:136
  113.7 0.1 copy.66
  113.8 0.1 copy.67
  113.9 6.9 %all-to-all-done = f32[32,1,256]{2,1,0:T(1,128)S(1)} async-done(((f32[32,1,256]{2,1,0:T(1,128)}), f32[32,1,256]{2,1,0:T(1,128)S(1)}, u32[]{:S(2)}, u32[]{:S(2)}) %all-to-all-start) | async-done | bytes 32800 | tf_op jit(solution)/shard_map/all_to_all | solution.py:20
  120.8 0.5 broadcast.173
  121.4 0.7 reduce.1
  122.1 0.1 reshape.213
  122.2 0.1 copy.64
  122.3 0.7 reshape.214
  123.0 3.8 %all-to-all-start.2 = ((f32[32,1,256]{2,1,0:T(1,128)}), f32[32,1,256]{2,1,0:T(1,128)S(1)}, u32[]{:S(2)}, u32[]{:S(2)}) async-start(f32[32,1,256]{2,1,0:T(1,128)} %reshape.214), calls=%async_computation.2 | async-start | bytes 65536 | tf_op jit(solution)/shard_map/all_to_all | solution.py:20
  126.8 0.7 fusion.25
  127.6 9.1 %all-to-all-done.2 = f32[32,1,256]{2,1,0:T(1,128)S(1)} async-done(((f32[32,1,256]{2,1,0:T(1,128)}), f32[32,1,256]{2,1,0:T(1,128)S(1)}, u32[]{:S(2)}, u32[]{:S(2)}) %all-to-all-start.2) | async-done | bytes 32800 | tf_op jit(solution)/shard_map/all_to_all | solution.py:20
  136.7 3.9 %all-to-all-start.1 = ((bf16[32,8,128]{2,1,0:T(8,128)(2,1)}), bf16[32,8,128]{2,1,0:T(8,128)(2,1)S(1)}, u32[]{:S(2)}, u32[]{:S(2)}) async-start(bf16[32,8,128]{2,1,0:T(8,128)(2,1)} %fusion.25), calls=%async_computation.1 | async-start | bytes 131072 | tf_op jit(solution)/shard_map/all_to_all | solution.py:38
  140.6 0.7 reduce.2
  141.3 0.1 reshape.215
  141.4 0.1 copy.68
  141.5 0.1 broadcast_bitcast_fusion
  141.6 9.0 %all-to-all-done.1 = bf16[32,8,128]{2,1,0:T(8,128)(2,1)S(1)} async-done(((bf16[32,8,128]{2,1,0:T(8,128)(2,1)}), bf16[32,8,128]{2,1,0:T(8,128)(2,1)S(1)}, u32[]{:S(2)}, u32[]{:S(2)}) %all-to-all-start.1) | async-done | bytes 65568 | tf_op jit(solution)/shard_map/all_to_all | solution.py:38
  150.6 0.0 copy-done.1
  150.6 0.2 fusion.15
  150.9 13.2 %all_to_all.36 = bf16[32,8,128]{2,1,0:T(8,128)(2,1)S(1)} all-to-all(bf16[32,8,128]{2,1,0:T(8,128)(2,1)S(1)} %fusion.15), channel_id=1, replica_groups=mesh['batch'=8,'cache'=32] {'cache'}, dimensions={0} | all-to-all | bytes 131072 | tf_op jit(solution)/shard_map/all_to_all | solution.py:38
  164.1 0.8 fusion.45
  164.9 0.6 broadcast_in_dim.83
  165.5 3.9 %all-to-all-start.4 = ((f32[32,1,8]{2,1,0:T(1,128)}), f32[32,1,8]{2,1,0:T(1,128)S(1)}, u32[]{:S(2)}, u32[]{:S(2)}) async-start(f32[32,1,8]{2,1,0:T(1,128)} %broadcast_in_dim.83), calls=%async_computation.4 | async-start | bytes 32768 | tf_op jit(solution)/shard_map/all_to_all | solution.py:20
  169.3 0.8 dynamic-slice_convert_fusion
  170.1 9.1 %all-to-all-done.4 = f32[32,1,8]{2,1,0:T(1,128)S(1)} async-done(((f32[32,1,8]{2,1,0:T(1,128)}), f32[32,1,8]{2,1,0:T(1,128)S(1)}, u32[]{:S(2)}, u32[]{:S(2)}) %all-to-all-start.4) | async-done | bytes 1056 | tf_op jit(solution)/shard_map/all_to_all | solution.py:20
  179.1 0.1 reduce_sum.78
  179.2 0.1 fusion.47
  179.3 13.0 %all_to_all.37 = bf16[32,8,128]{2,1,0:T(8,128)(2,1)S(1)} all-to-all(bf16[32,8,128]{2,1,0:T(8,128)(2,1)S(1)} %broadcast_in_dim.84), channel_id=1, replica_groups=mesh['batch'=8,'cache'=32] {'cache'}, dimensions={0} | all-to-all | bytes 131072 | tf_op jit(solution)/shard_map/all_to_all | solution.py:20
  192.3 2.1 fusion.28
  194.3 3.4 %fusion.16 = bf16[32,8,128]{2,1,0:T(8,128)(2,1)S(1)} fusion(bf16[224,4096]{1,0:T(8,128)(2,1)} %param.27, bf16[4096,224]{0,1:T(8,128)(2,1)} %param.26, bf16[32,8,128]{2,1,0:T(8,128)(2,1)S(1)} %all_to_all.37, f32[8,224]{1,0:T(8,128)S(1)} %fusion.28), kind=kOutput, calls=%fused_computation.12 | convolution fusion | flops 29403648 | bytes 3808256 | tf_op jit(solution)/shard_map/dot_general | solution.py:175
  197.8 13.2 %all_to_all.38 = bf16[32,8,128]{2,1,0:T(8,128)(2,1)S(1)} all-to-all(bf16[32,8,128]{2,1,0:T(8,128)(2,1)S(1)} %fusion.16), channel_id=1, replica_groups=mesh['batch'=8,'cache'=32] {'cache'}, dimensions={0} | all-to-all | bytes 131072 | tf_op jit(solution)/shard_map/all_to_all | solution.py:38
  211.0 0.6 fusion.48
  (21 shorter events, 0.4 us)
Async XLA Ops:
  0.0 102.9 %copy-start = (bf16[8,128,1024]{2,1,0:T(8,128)(2,1)S(1)}, bf16[8,128,1024]{2,1,0:T(8,128)(2,1)}, u32[]{:S(2)}) copy-start(bf16[8,128,1024]{2,1,0:T(8,128)(2,1)} %param.19) | copy-start | bytes 6291460
  0.0 102.5 %copy-start.2 = (s32[8]{0:T(128)S(1)}, s32[8]{0:T(128)}, u32[]{:S(2)}) copy-start(s32[8]{0:T(128)} %param.22) | copy-start | bytes 100
  105.2 15.6 %all-to-all-start = ((f32[32,1,256]{2,1,0:T(1,128)}), f32[32,1,256]{2,1,0:T(1,128)S(1)}, u32[]{:S(2)}, u32[]{:S(2)}) async-start(f32[32,1,256]{2,1,0:T(1,128)} %reshape.212), calls=%async_computation | async-start | bytes 65536 | tf_op jit(solution)/shard_map/all_to_all | solution.py:20
  111.3 39.3 %copy-start.1 = (bf16[128,4096]{1,0:T(8,128)(2,1)S(1)}, bf16[128,4096]{1,0:T(8,128)(2,1)}, u32[]{:S(2)}) copy-start(bf16[128,4096]{1,0:T(8,128)(2,1)} %param.23) | copy-start | bytes 3145732
  123.0 13.7 %all-to-all-start.2 = ((f32[32,1,256]{2,1,0:T(1,128)}), f32[32,1,256]{2,1,0:T(1,128)S(1)}, u32[]{:S(2)}, u32[]{:S(2)}) async-start(f32[32,1,256]{2,1,0:T(1,128)} %reshape.214), calls=%async_computation.2 | async-start | bytes 65536 | tf_op jit(solution)/shard_map/all_to_all | solution.py:20
  136.7 13.9 %all-to-all-start.1 = ((bf16[32,8,128]{2,1,0:T(8,128)(2,1)}), bf16[32,8,128]{2,1,0:T(8,128)(2,1)S(1)}, u32[]{:S(2)}, u32[]{:S(2)}) async-start(bf16[32,8,128]{2,1,0:T(8,128)(2,1)} %fusion.25), calls=%async_computation.1 | async-start | bytes 131072 | tf_op jit(solution)/shard_map/all_to_all | solution.py:38
  165.5 13.7 %all-to-all-start.4 = ((f32[32,1,8]{2,1,0:T(1,128)}), f32[32,1,8]{2,1,0:T(1,128)S(1)}, u32[]{:S(2)}, u32[]{:S(2)}) async-start(f32[32,1,8]{2,1,0:T(1,128)} %broadcast_in_dim.83), calls=%async_computation.4 | async-start | bytes 32768 | tf_op jit(solution)/shard_map/all_to_all | solution.py:20
where the time goes:
time: 212 us
  blocking collectives  134 us (63%)
  waiting for transfers between devices  34.1 us (16%)
  starting transfers between devices  17.2 us (8%)
  matrix products  13.7 us (6%)
  other arithmetic  8.78 us (4%)
  local copies, waits for them, and re-layouts  3.68 us (2%)
    all_gather x1, blocking collectives, per_device(): lax.all_gather(query_slice, 'cache', axis=1, tiled=True)  52.3 us
    all_gather x1, blocking collectives, sent_together(): out = lax.all_gather(both, axis, axis=dim, tiled=True)  42.2 us
    all_to_all x2, blocking collectives, sum_at_owner(): parts = lax.all_to_all(cut_along(x, dim, devices), axis, 0, 0, tiled=True)  26.3 us
    all_to_all x3, waiting for transfers between devices, sent_to_all(): return lax.all_to_all(copies, axis, split_axis=0, concat_axis=0, tiled=True)  25.1 us
    all_to_all x3, starting transfers between devices, sent_to_all(): return lax.all_to_all(copies, axis, split_axis=0, concat_axis=0, tiled=True)  13.3 us
    all_to_all x1, blocking collectives, sent_to_all(): return lax.all_to_all(copies, axis, split_axis=0, concat_axis=0, tiled=True)  13 us
    all_to_all x1, waiting for transfers between devices, sum_at_owner(): parts = lax.all_to_all(cut_along(x, dim, devices), axis, 0, 0, tiled=True)  8.97 us
  transfers between devices with their start and end apart: 4, of which 4 were waited for; matrix products, arithmetic and copies ran while one was open for 3% of the time, Pallas kernels for 0%

commit v1 on v0

--- a/solution.py
+++ b/solution.py
@@ -6,6 +6,11 @@
 HEADS = 32
 KV_HEADS = 8
 HEAD_DIM = 128
+
+
+def gather_by_exchange(x, axis, dim):
+    copies = jnp.concatenate([x] * lax.axis_size(axis), axis=dim)
+    return lax.all_to_all(copies, axis, dim, dim, tiled=True)
 
 
 def sent_together(arrays, axis, dim, along):
@@ -99,7 +104,7 @@
     key_part = jnp.dot(normed, w_key, preferred_element_type=jnp.float32).astype(jnp.bfloat16)
     value_part = jnp.dot(normed, w_value, preferred_element_type=jnp.float32).astype(jnp.bfloat16)
     query_raw, key_raw, value_new = (
-        lax.all_gather(query_slice, "cache", axis=1, tiled=True),
+        gather_by_exchange(query_slice, "cache", 1),
         *sent_together((key_part, value_part), "cache", 1, 0),
     )
     query = rotate(query_raw.astype(jnp.float32).reshape(seqs, HEADS, HEAD_DIM), write_pos).astype(

time: 212 us -> 194 us (0.915)
  blocking collectives: 134 us -> 83.4 us
  local copies, waits for them, and re-layouts: 3.68 us -> 22.3 us
  starting transfers between devices: 17.2 us -> 30 us
    all_gather x1 -> x0, blocking collectives: 52.3 us -> none  [per_device(): lax.all_gather(query_slice, 'cache', axis=1, tiled=True)]
    unnamed x11 -> x43, local copies, waits for them, and re-layouts: 1.79 us -> 19.2 us
    all_to_all x0 -> x1, starting transfers between devices: none -> 11.5 us  [gather_by_exchange(): return lax.all_to_all(copies, axis, dim, dim, tiled=True)]
  transfers between devices with their start and end apart: 4 -> 5, of which waited for: 4 -> 4; matrix products, arithmetic and copies ran while one was open for 3% -> 5% of each run, Pallas kernels for 0% -> 0%
where the time goes in v1:
time: 194 us; the launch traced here: 193 us
  blocking collectives  83.4 us (43%)
  waiting for transfers between devices  34.6 us (18%)
  starting transfers between devices  30 us (15%)
  local copies, waits for them, and re-layouts  22.3 us (11%)
  matrix products  14.3 us (7%)
  other arithmetic  8.22 us (4%)
    all_gather x1, blocking collectives, sent_together(): out = lax.all_gather(both, axis, axis=dim, tiled=True)  44.1 us
    all_to_all x2, blocking collectives, sum_at_owner(): parts = lax.all_to_all(cut_along(x, dim, devices), axis, 0, 0, tiled=True)  26.2 us
    all_to_all x3, waiting for transfers between devices, sent_to_all(): return lax.all_to_all(copies, axis, split_axis=0, concat_axis=0, tiled=True)  25.6 us
    unnamed x43, local copies, waits for them, and re-layouts  19.2 us
    all_to_all x3, starting transfers between devices, sent_to_all(): return lax.all_to_all(copies, axis, split_axis=0, concat_axis=0, tiled=True)  14.6 us
    all_to_all x1, blocking collectives, sent_to_all(): return lax.all_to_all(copies, axis, split_axis=0, concat_axis=0, tiled=True)  13.2 us
    all_to_all x1, starting transfers between devices, gather_by_exchange(): return lax.all_to_all(copies, axis, dim, dim, tiled=True)  11.5 us
    all_to_all x1, waiting for transfers between devices, sum_at_owner(): parts = lax.all_to_all(cut_along(x, dim, devices), axis, 0, 0, tiled=True)  9.06 us
  transfers between devices with their start and end apart: 5, of which 4 were waited for; matrix products, arithmetic and copies ran while one was open for 5% of the time, Pallas kernels for 0%

profile of v1, /device:TPU:4, one launch (start us, length us, event | category | flops | bytes accessed | tf_op | source)
XLA Modules:
  0.0 193.1 jit_solution(954151615337496523)
XLA Ops:
  0.0 1.2 fusion.18
  1.2 0.7 convert_element_type.95
  1.9 2.2 %constant_dynamic-update-slice_fusion.31 = (bf16[8,4096]{1,0:T(8,128)(2,1)}, bf16[8,128]{1,0:T(8,128)(2,1)S(1)}) fusion(bf16[4096,128]{1,0:T(8,128)(2,1)} %param.16, bf16[8,4096]{1,0:T(8,128)(2,1)} %param.14, f32[4096]{0:T(1024)S(1)} %convert_element_type.95, f32[8]{0:T(128)S(1)} %add_rsqrt_fusion.1), kind=kOutput, calls=%fused_computation.64 | convolution fusion | flops 8520703 | bytes 1134624 | tf_op jit(solution)/shard_map/dot_general | solution.py:103
  4.0 0.6 constant_dynamic-update-slice_fusion.30
  4.6 0.6 constant_dynamic-update-slice_fusion.29
  5.2 0.6 constant_dynamic-update-slice_fusion.28
  5.8 0.6 constant_dynamic-update-slice_fusion.27
  6.4 0.6 constant_dynamic-update-slice_fusion.26
  7.0 0.6 constant_dynamic-update-slice_fusion.25
  7.5 0.6 constant_dynamic-update-slice_fusion.24
  8.1 0.6 constant_dynamic-update-slice_fusion.23
  8.7 0.6 constant_dynamic-update-slice_fusion.22
  9.3 0.6 constant_dynamic-update-slice_fusion.21
  9.8 0.6 constant_dynamic-update-slice_fusion.20
  10.4 0.6 constant_dynamic-update-slice_fusion.19
  11.0 0.6 constant_dynamic-update-slice_fusion.18
  11.6 0.6 constant_dynamic-update-slice_fusion.17
  12.2 0.6 constant_dynamic-update-slice_fusion.16
  12.8 0.6 constant_dynamic-update-slice_fusion.15
  13.3 0.6 constant_dynamic-update-slice_fusion.14
  13.9 0.6 constant_dynamic-update-slice_fusion.13
  14.5 0.6 constant_dynamic-update-slice_fusion.12
  15.1 0.6 constant_dynamic-update-slice_fusion.11
  15.7 0.6 constant_dynamic-update-slice_fusion.10
  16.3 0.6 constant_dynamic-update-slice_fusion.9
  16.8 0.6 constant_dynamic-update-slice_fusion.8
  17.4 0.6 constant_dynamic-update-slice_fusion.7
  18.0 0.6 constant_dynamic-update-slice_fusion.6
  18.6 0.6 constant_dynamic-update-slice_fusion.5
  19.2 0.6 constant_dynamic-update-slice_fusion.4
  19.8 0.6 constant_dynamic-update-slice_fusion.3
  20.4 0.6 constant_dynamic-update-slice_fusion.2
  20.9 0.6 constant_dynamic-update-slice_fusion.1
  21.5 0.6 constant_dynamic-update-slice_fusion
  22.1 11.5 %all-to-all-start = ((bf16[8,32,128]{2,0,1:T(8,128)(2,1)}), bf16[8,32,128]{2,0,1:T(8,128)(2,1)S(1)}, u32[]{:S(2)}, u32[]{:S(2)}) async-start(bf16[8,32,128]{2,0,1:T(8,128)(2,1)} %bitcast), calls=%async_computation | async-start | bytes 131072 | tf_op jit(solution)/shard_map/all_to_all | solution.py:13
  33.6 0.7 fusion.62
  34.3 1.2 convolution_convert_fusion.3
  35.6 1.2 convolution_convert_fusion.2
  36.8 44.1 %all-gather = bf16[32,32,16]{1,2,0:T(8,128)(2,1)S(1)} all-gather(bf16[1,32,16]{1,2,0:T(8,128)(2,1)S(1)} %maximum_bitcast_fusion.1), channel_id=1, replica_groups=mesh['batch'=8,'cache'=32] {'cache'}, dimensions={0}, use_global_device_ids=true | all-gather | bytes 33792 | tf_op jit(solution)/shard_map/all_gather | solution.py:19
  81.4 0.6 copy.60
  82.6 1.3 fusion.63
  84.6 0.7 reshape.205
  85.3 7.0 %all-to-all-start.1 = ((f32[32,1,256]{2,1,0:T(1,128)}), f32[32,1,256]{2,1,0:T(1,128)S(1)}, u32[]{:S(2)}, u32[]{:S(2)}) async-start(f32[32,1,256]{2,1,0:T(1,128)} %reshape.205), calls=%async_computation.1 | async-start | bytes 65536 | tf_op jit(solution)/shard_map/all_to_all | solution.py:25
  92.3 2.4 %fusion.12 = f32[8,8,4,128]{3,2,1,0:T(4,128)S(1)} fusion(f32[8,8,4,128]{3,2,1,0:T(4,128)S(1)} %get-tuple-element.24, f32[8,8,128]{2,1,0:T(8,128)} %copy.60, f32[8,8,4]{2,1,0:T(8,128)S(1)} %convert_element_type.104, f32[8,8,4]{2,1,0:T(8,128)S(1)} %fusion.35, pred[8,128]{1,0:T(8,128)(4,1)S(1)} %fusion.44, bf16[8,128,1024]{2,1,0:T(8,128)(2,1)} %param.20), kind=kOutput, calls=%fused_computation.10 | convolution fusion | flops 8552448 | bytes 2395136 | tf_op jit(solution)/shard_map/bkgw,bwkd->bkgd/dot_general | solution.py:141
  94.9 7.3 %all-to-all-done.1 = f32[32,1,256]{2,1,0:T(1,128)S(1)} async-done(((f32[32,1,256]{2,1,0:T(1,128)}), f32[32,1,256]{2,1,0:T(1,128)S(1)}, u32[]{:S(2)}, u32[]{:S(2)}) %all-to-all-start.1) | async-done | bytes 32800 | tf_op jit(solution)/shard_map/all_to_all | solution.py:25
  102.7 0.7 reduce.1
  103.7 0.7 reshape.207
  104.4 3.8 %all-to-all-start.3 = ((f32[32,1,256]{2,1,0:T(1,128)}), f32[32,1,256]{2,1,0:T(1,128)S(1)}, u32[]{:S(2)}, u32[]{:S(2)}) async-start(f32[32,1,256]{2,1,0:T(1,128)} %reshape.207), calls=%async_computation.3 | async-start | bytes 65536 | tf_op jit(solution)/shard_map/all_to_all | solution.py:25
  108.2 0.7 fusion.25
  108.9 9.2 %all-to-all-done.3 = f32[32,1,256]{2,1,0:T(1,128)S(1)} async-done(((f32[32,1,256]{2,1,0:T(1,128)}), f32[32,1,256]{2,1,0:T(1,128)S(1)}, u32[]{:S(2)}, u32[]{:S(2)}) %all-to-all-start.3) | async-done | bytes 32800 | tf_op jit(solution)/shard_map/all_to_all | solution.py:25
  118.1 3.9 %all-to-all-start.2 = ((bf16[32,8,128]{2,1,0:T(8,128)(2,1)}), bf16[32,8,128]{2,1,0:T(8,128)(2,1)S(1)}, u32[]{:S(2)}, u32[]{:S(2)}) async-start(bf16[32,8,128]{2,1,0:T(8,128)(2,1)} %fusion.25), calls=%async_computation.2 | async-start | bytes 131072 | tf_op jit(solution)/shard_map/all_to_all | solution.py:43
  122.0 0.7 reduce.2
  123.0 9.1 %all-to-all-done.2 = bf16[32,8,128]{2,1,0:T(8,128)(2,1)S(1)} async-done(((bf16[32,8,128]{2,1,0:T(8,128)(2,1)}), bf16[32,8,128]{2,1,0:T(8,128)(2,1)S(1)}, u32[]{:S(2)}, u32[]{:S(2)}) %all-to-all-start.2) | async-done | bytes 65568 | tf_op jit(solution)/shard_map/all_to_all | solution.py:43
  132.4 13.1 %all_to_all.45 = bf16[32,8,128]{2,1,0:T(8,128)(2,1)S(1)} all-to-all(bf16[32,8,128]{2,1,0:T(8,128)(2,1)S(1)} %fusion.15), channel_id=1, replica_groups=mesh['batch'=8,'cache'=32] {'cache'}, dimensions={0} | all-to-all | bytes 131072 | tf_op jit(solution)/shard_map/all_to_all | solution.py:43
  145.5 0.8 fusion.45
  146.3 0.6 broadcast_in_dim.83
  146.9 3.9 %all-to-all-start.5 = ((f32[32,1,8]{2,1,0:T(1,128)}), f32[32,1,8]{2,1,0:T(1,128)S(1)}, u32[]{:S(2)}, u32[]{:S(2)}) async-start(f32[32,1,8]{2,1,0:T(1,128)} %broadcast_in_dim.83), calls=%async_computation.5 | async-start | bytes 32768 | tf_op jit(solution)/shard_map/all_to_all | solution.py:25
  150.7 0.8 dynamic-slice_convert_fusion
  151.5 9.1 %all-to-all-done.5 = f32[32,1,8]{2,1,0:T(1,128)S(1)} async-done(((f32[32,1,8]{2,1,0:T(1,128)}), f32[32,1,8]{2,1,0:T(1,128)S(1)}, u32[]{:S(2)}, u32[]{:S(2)}) %all-to-all-start.5) | async-done | bytes 1056 | tf_op jit(solution)/shard_map/all_to_all | solution.py:25
  160.7 13.2 %all_to_all.46 = bf16[32,8,128]{2,1,0:T(8,128)(2,1)S(1)} all-to-all(bf16[32,8,128]{2,1,0:T(8,128)(2,1)S(1)} %broadcast_in_dim.84), channel_id=1, replica_groups=mesh['batch'=8,'cache'=32] {'cache'}, dimensions={0} | all-to-all | bytes 131072 | tf_op jit(solution)/shard_map/all_to_all | solution.py:25
  173.9 2.1 %fusion.28 = f32[8,224]{1,0:T(8,128)S(1)} fusion(bf16[4096,224]{0,1:T(8,128)(2,1)} %param.25, bf16[32,8,128]{2,1,0:T(8,128)(2,1)S(1)} %all_to_all.46), kind=kOutput, calls=%fused_computation.68 | convolution fusion | flops 14680064 | bytes 1907712 | tf_op jit(solution)/shard_map/dot_general | solution.py:177
  176.0 3.4 %fusion.16 = bf16[32,8,128]{2,1,0:T(8,128)(2,1)S(1)} fusion(bf16[224,4096]{1,0:T(8,128)(2,1)} %param.27, bf16[4096,224]{0,1:T(8,128)(2,1)} %param.26, bf16[32,8,128]{2,1,0:T(8,128)(2,1)S(1)} %all_to_all.46, f32[8,224]{1,0:T(8,128)S(1)} %fusion.28), kind=kOutput, calls=%fused_computation.12 | convolution fusion | flops 29403648 | bytes 3808256 | tf_op jit(solution)/shard_map/dot_general | solution.py:180
  179.4 13.1 %all_to_all.47 = bf16[32,8,128]{2,1,0:T(8,128)(2,1)S(1)} all-to-all(bf16[32,8,128]{2,1,0:T(8,128)(2,1)S(1)} %fusion.16), channel_id=1, replica_groups=mesh['batch'=8,'cache'=32] {'cache'}, dimensions={0} | all-to-all | bytes 131072 | tf_op jit(solution)/shard_map/all_to_all | solution.py:43
  192.6 0.6 fusion.48
  (53 shorter events, 3.4 us)
Async XLA Ops:
  0.0 82.5 %copy-start = (bf16[8,128,1024]{2,1,0:T(8,128)(2,1)S(1)}, bf16[8,128,1024]{2,1,0:T(8,128)(2,1)}, u32[]{:S(2)}) copy-start(bf16[8,128,1024]{2,1,0:T(8,128)(2,1)} %param.19) | copy-start | bytes 6291460
  0.0 81.4 %copy-start.3 = (s32[8]{0:T(128)S(1)}, s32[8]{0:T(128)}, u32[]{:S(2)}) copy-start(s32[8]{0:T(128)} %param.21) | copy-start | bytes 100
  0.0 81.2 %copy-start.2 = (s32[8]{0:T(128)S(1)}, s32[8]{0:T(128)}, u32[]{:S(2)}) copy-start(s32[8]{0:T(128)} %param.22) | copy-start | bytes 100
  22.1 60.0 %all-to-all-start = ((bf16[8,32,128]{2,0,1:T(8,128)(2,1)}), bf16[8,32,128]{2,0,1:T(8,128)(2,1)S(1)}, u32[]{:S(2)}, u32[]{:S(2)}) async-start(bf16[8,32,128]{2,0,1:T(8,128)(2,1)} %bitcast), calls=%async_computation | async-start | bytes 131072 | tf_op jit(solution)/shard_map/all_to_all | solution.py:13
  85.3 16.9 %all-to-all-start.1 = ((f32[32,1,256]{2,1,0:T(1,128)}), f32[32,1,256]{2,1,0:T(1,128)S(1)}, u32[]{:S(2)}, u32[]{:S(2)}) async-start(f32[32,1,256]{2,1,0:T(1,128)} %reshape.205), calls=%async_computation.1 | async-start | bytes 65536 | tf_op jit(solution)/shard_map/all_to_all | solution.py:25
  92.3 39.9 %copy-start.1 = (bf16[128,4096]{1,0:T(8,128)(2,1)S(1)}, bf16[128,4096]{1,0:T(8,128)(2,1)}, u32[]{:S(2)}) copy-start(bf16[128,4096]{1,0:T(8,128)(2,1)} %param.23) | copy-start | bytes 3145732
  104.4 13.7 %all-to-all-start.3 = ((f32[32,1,256]{2,1,0:T(1,128)}), f32[32,1,256]{2,1,0:T(1,128)S(1)}, u32[]{:S(2)}, u32[]{:S(2)}) async-start(f32[32,1,256]{2,1,0:T(1,128)} %reshape.207), calls=%async_computation.3 | async-start | bytes 65536 | tf_op jit(solution)/shard_map/all_to_all | solution.py:25
  118.1 14.0 %all-to-all-start.2 = ((bf16[32,8,128]{2,1,0:T(8,128)(2,1)}), bf16[32,8,128]{2,1,0:T(8,128)(2,1)S(1)}, u32[]{:S(2)}, u32[]{:S(2)}) async-start(bf16[32,8,128]{2,1,0:T(8,128)(2,1)} %fusion.25), calls=%async_computation.2 | async-start | bytes 131072 | tf_op jit(solution)/shard_map/all_to_all | solution.py:43
  146.9 13.7 %all-to-all-start.5 = ((f32[32,1,8]{2,1,0:T(1,128)}), f32[32,1,8]{2,1,0:T(1,128)S(1)}, u32[]{:S(2)}, u32[]{:S(2)}) async-start(f32[32,1,8]{2,1,0:T(1,128)} %broadcast_in_dim.83), calls=%async_computation.5 | async-start | bytes 32768 | tf_op jit(solution)/shard_map/all_to_all | solution.py:25
